TPU v7x, 32 devices: a whole 2x2x4 slice. The times are simulated.
32 devices in a mesh: dp: 2 (over y), seq: 16 (over z, x, core).
Axes of the slice: x: 2, y: 2, z: 4, core: 2. Of those that a mesh axis runs over, the one named last changes fastest.
Arguments:
- hidden_in: bfloat16 [2, 1024, 2048], P('dp', 'seq'), may hold values from -6 to 6
- attn_gain: float32 [2048], replicated, may hold values from 0.1 to 1.9
- w_query: bfloat16 [2048, 1280], P('dp'), may hold values from -2 to 2
- w_keyval: bfloat16 [2048, 512], P('dp'), may hold values from -1 to 1
- w_output: bfloat16 [1280, 2048], P(None, 'dp'), may hold values from -0.15625 to 0.15625
- post_gain: float32 [2048], replicated, may hold values from 0.1 to 1.9
Outputs:
- hidden_out: bfloat16 [2, 1024, 2048], P('dp', 'seq')
All inputs are finite; a program needn't handle non-finite values.
Results may differ from a plain program's by a relative error of at most 0.009.
Values may be sent and summed in bfloat16 or wider, within the bound.
No kernel may reach another device: no remote copies, remote signals or barrier semaphores. Data moves between devices by JAX's collectives and lax.ppermute only.
A program may use at most 64 MiB of HBM per device.

v0:
```python
import jax
import jax.numpy as jnp
from jax import lax
from jax.sharding import PartitionSpec as P


def rms_norm(v, gain):
    v = v.astype(jnp.float32)
    return v * lax.rsqrt(jnp.mean(v * v, axis=-1, keepdims=True) + 1e-06) * gain


def rotary(t, positions):
    half = t.shape[-1] // 2
    freq = jnp.exp(-jnp.log(10000.0) * jnp.arange(half, dtype=jnp.float32) * 2.0 / t.shape[-1])
    angle = positions.astype(jnp.float32)[:, None, None] * freq[None, None, :]
    cosine = jnp.cos(angle)
    sine = jnp.sin(angle)
    first = t[..., :half]
    second = t[..., half:]
    return jnp.concatenate(
        [first * cosine - second * sine, second * cosine + first * sine], axis=-1
    )


def local(hidden_in, attn_gain, w_query, w_keyval, w_output, post_gain):
    frame = hidden_in[0]
    count = frame.shape[0]
    head_dim = w_keyval.shape[1] // 2
    width_q = w_query.shape[1]
    num_heads = width_q // head_dim
    normed = rms_norm(frame, attn_gain).astype(jnp.bfloat16)
    slices = lax.all_to_all(normed, "dp", split_axis=1, concat_axis=0, tiled=True)
    joined = jnp.concatenate([w_query, w_keyval], axis=1)
    summed = lax.psum_scatter(
        jnp.dot(slices, joined, preferred_element_type=jnp.float32),
        "dp",
        scatter_dimension=0,
        tiled=True,
    )
    query_raw = summed[:, :width_q]
    keyval_raw = summed[:, width_q:]
    positions = lax.axis_index("seq") * count + jnp.arange(count, dtype=jnp.int32)
    query = (
        rotary(query_raw.reshape(count, num_heads, head_dim), positions) * head_dim ** (-0.5)
    ).astype(jnp.bfloat16)
    keys = rotary(keyval_raw[:, None, :head_dim], positions)[:, 0, :].astype(jnp.bfloat16)
    values = keyval_raw[:, head_dim:].astype(jnp.bfloat16)
    stacked = jnp.transpose(query, (1, 0, 2)).reshape(num_heads * count, head_dim)
    rows_all = num_heads * count
    running_max = jnp.full((rows_all,), -1e30, jnp.float32)
    key_piece = lax.all_gather(keys, "seq", axis=0, tiled=True)
    value_piece = lax.all_gather(values, "seq", axis=0, tiled=True)
    scores = lax.dot_general(
        stacked, key_piece, (((1,), (1,)), ((), ())), preferred_element_type=jnp.float32
    )
    new_max = jnp.maximum(running_max, jnp.max(scores, axis=1))
    expo = jnp.exp(scores - new_max[:, None])
    new_total = jnp.sum(expo, axis=1)
    new_sum = jnp.dot(expo.astype(jnp.bfloat16), value_piece, preferred_element_type=jnp.float32)
    heads = (new_sum / new_total[:, None]).reshape(num_heads, count, head_dim)
    attended = jnp.transpose(heads, (1, 0, 2)).reshape(count, width_q).astype(jnp.bfloat16)
    episode_parts = jnp.dot(
        lax.all_gather(attended, "dp", axis=0, tiled=True),
        w_output,
        preferred_element_type=jnp.float32,
    )
    projected = lax.all_to_all(
        episode_parts.astype(jnp.bfloat16), "dp", split_axis=0, concat_axis=1, tiled=True
    ).astype(episode_parts.dtype)
    result = frame.astype(jnp.float32) + rms_norm(projected, post_gain)
    return result.astype(jnp.bfloat16)[None]


def solution(mesh):
    in_specs = (P("dp", "seq", None), P(), P("dp", None), P("dp", None), P(None, "dp"), P())
    out_specs = P("dp", "seq", None)
    return jax.shard_map(local, mesh=mesh, in_specs=in_specs, out_specs=out_specs, check_vma=False)
```

profile of v0, /device:TPU:0, one launch (start us, length us, event | category | flops | bytes accessed | tf_op | source)
XLA Modules:
  0.0 116.7 jit_solution(12723673413298586071)
XLA Ops:
  6.5 0.0 copy-start
  6.5 0.0 reduce-scatter.2.cloned.1.call-start
  6.5 1.6 %reshape.228 = f32[64,2,1024]{2,1,0:T(2,128)S(1)} reshape(bf16[1,64,2048]{2,1,0:T(8,128)(2,1)} %param.6) | data formatting | bytes 786432 | tf_op jit(solution)/shard_map/convert_element_type | solution.py:70
  8.2 1.1 multiply_reduce_fusion
  9.3 0.7 mul.156
  10.0 0.3 multiply_convert_fusion
  10.4 9.2 %all_to_all.29 = bf16[64,2,1024]{2,0,1:T(8,128)(2,1)S(1)} all-to-all(bf16[64,2,1024]{2,0,1:T(8,128)(2,1)S(1)} %copy.15), channel_id=1, replica_groups=mesh['dp'=2,'seq'=16] {'dp'}, dimensions={1} | all-to-all | bytes 524288 | tf_op jit(solution)/shard_map/all_to_all | solution.py:32
  19.6 3.7 %fusion = f32[128,1792]{1,0:T(8,128)} fusion(bf16[128,1024]{1,0:T(8,128)(2,1)S(1)} %bitcast.30, bf16[1024,512]{1,0:T(8,128)(2,1)} %param.9, bf16[1024,1280]{1,0:T(8,128)(2,1)} %param.8), kind=kOutput, calls=%fused_computation | convolution fusion | flops 477102080 | bytes 4849664 | tf_op jit(solution)/shard_map/dot_general | solution.py:35
  23.3 0.0 reduce-scatter.2.cloned.1.call-update
  23.3 0.2 multiply_cosine_fusion.1
  23.5 19.2 %reduce-scatter.2.cloned.1.call-done = f32[64,1792]{1,0:T(8,128)} async-done(((f32[128,1792]{1,0:T(8,128)}), f32[64,1792]{1,0:T(8,128)}) %reduce-scatter.2.cloned.1.call-update) | async-done | bytes 458768 | tf_op jit(solution)/shard_map/reduce_scatter | solution.py:34
  42.7 1.0 slice.32
  43.7 0.1 reshape.226
  43.8 0.1 multiply_subtract_fusion
  43.9 0.1 fusion.13
  44.0 0.8 slice_bitcast_fusion
  44.9 0.2 fusion.19
  45.1 22.9 %all-gather = bf16[1024,1,256]{2,0,1:T(8,128)(2,1)S(1)} all-gather(bf16[64,1,256]{2,0,1:T(8,128)(2,1)S(1)} %pad_maximum_fusion), channel_id=2, replica_groups=mesh['dp'=2,'seq'=16] {'seq'}, dimensions={0}, use_global_device_ids=true | all-gather | bytes 557056 | tf_op jit(solution)/shard_map/all_gather | solution.py:51
  68.0 0.5 fusion.23
  68.4 0.8 slice.49
  69.3 18.9 %all_gather.10 = bf16[1024,256]{1,0:T(8,128)(2,1)S(1)} all-gather(bf16[64,256]{1,0:T(8,128)(2,1)S(1)} %slice.49), channel_id=1, replica_groups=mesh['dp'=2,'seq'=16] {'seq'}, dimensions={0}, use_global_device_ids=true | all-gather | bytes 557056 | tf_op jit(solution)/shard_map/all_gather | solution.py:52
  88.1 0.4 fusion.5
  88.5 0.4 fusion.4
  88.9 7.1 %all_gather.11 = bf16[128,1280]{1,0:T(8,128)(2,1)S(1)} all-gather(bf16[64,1280]{1,0:T(8,128)(2,1)S(1)} %bitcast.29), channel_id=1, replica_groups=mesh['dp'=2,'seq'=16] {'dp'}, dimensions={0}, use_global_device_ids=true | all-gather | bytes 491520 | tf_op jit(solution)/shard_map/all_gather | solution.py:63
  96.0 0.0 copy-done
  96.0 0.5 convolution_convert_fusion
  96.5 0.0 copy-start.1
  96.6 0.0 copy-start.2
  96.6 7.7 %all_to_all.30 = bf16[2,64,1024]{2,1,0:T(8,128)(2,1)S(1)} all-to-all(bf16[2,64,1024]{2,1,0:T(8,128)(2,1)S(1)} %bitcast.27), channel_id=1, replica_groups=mesh['dp'=2,'seq'=16] {'dp'}, dimensions={0} | all-to-all | bytes 524288 | tf_op jit(solution)/shard_map/all_to_all | solution.py:67
  104.3 1.2 %copy.18 = f32[64,2,1024]{2,1,0:T(2,128)} copy(f32[64,2,1024]{2,0,1:T(8,128)S(1)} %convert_bitcast_fusion) | data formatting | bytes 1048576 | tf_op jit(solution)/shard_map/convert_element_type | solution.py:69
  105.5 2.3 %reshape.229 = f32[1,64,2048]{2,1,0:T(8,128)} reshape(f32[64,2,1024]{2,1,0:T(2,128)} %copy.18) | data formatting | bytes 1048576 | tf_op jit(solution)/shard_map/convert_element_type | solution.py:69
  107.8 0.2 fusion.9
  108.0 0.0 copy-done.1
  108.0 0.0 copy-done.2
  108.0 1.9 %add_convert_fusion = bf16[1,64,2048]{2,1,0:T(8,128)(2,1)} fusion(f32[1,64,2048]{2,1,0:T(8,128)} %reshape.229, f32[2048]{0:T(1024)S(1)} %copy-done.2, f32[64]{0:T(128)S(1)} %add_rsqrt_fusion, bf16[1,64,2048]{2,1,0:T(8,128)(2,1)S(1)} %copy-done.1), kind=kLoop, calls=%fused_computation.18 | loop fusion | flops 655360 | bytes 1057024 | tf_op jit(solution)/shard_map/convert_element_type | solution.py:71
  (10 shorter events, 0.2 us)
Async XLA Ops:
  6.5 89.5 %copy-start = (bf16[1280,1024]{1,0:T(8,128)(2,1)S(1)}, bf16[1280,1024]{1,0:T(8,128)(2,1)}, u32[]{:S(2)}) copy-start(bf16[1280,1024]{1,0:T(8,128)(2,1)} %param.10) | copy-start | bytes 7864324
  6.5 36.2 %reduce-scatter.2.cloned.1.call-start = ((), (), s32[]{:S(2)}) async-start(), calls=%async_computation.3 | async-start | bytes 1376256 | tf_op jit(solution)/shard_map/reduce_scatter | solution.py:34
  96.5 11.4 %copy-start.1 = (bf16[1,64,2048]{2,1,0:T(8,128)(2,1)S(1)}, bf16[1,64,2048]{2,1,0:T(8,128)(2,1)}, u32[]{:S(2)}) copy-start(bf16[1,64,2048]{2,1,0:T(8,128)(2,1)} %param.6) | copy-start | bytes 786436
  96.6 11.4 %copy-start.2 = (f32[2048]{0:T(1024)S(1)}, f32[2048]{0:T(1024)}, u32[]{:S(2)}) copy-start(f32[2048]{0:T(1024)} %param.11) | copy-start | bytes 24580
Sparse Core Ops, SparseCore 0:
  23.4 19.2 reduce-scatter.1
where the time goes:
time: 117 us
  blocking collectives  65.8 us (56%)
  waiting for transfers between devices  19.2 us (16%)
  between operations  13.6 us (12%)
  local copies, waits for them, and re-layouts  8.72 us (7%)
  matrix products  5.02 us (4%)
  other arithmetic  4.41 us (4%)
    all_gather x1, blocking collectives, local(): key_piece = lax.all_gather(keys, 'seq', axis=0, tiled=True)  22.9 us
    reduce_scatter x1, waiting for transfers between devices, local(): lax.psum_scatter(jnp.dot(slices, joined, preferred_element_type=jnp.float...  19.2 us
    all_gather x1, blocking collectives, local(): value_piece = lax.all_gather(values, 'seq', axis=0, tiled=True)  18.9 us
    all_to_all x1, blocking collectives, local(): lax.all_to_all(normed, 'dp', split_axis=1, concat_axis=0, tiled=True)  9.24 us
    all_to_all x1, blocking collectives, local(): lax.all_to_all(episode_parts.astype(jnp.bfloat16), 'dp', split_axis=0, co...  7.69 us
    all_gather x1, blocking collectives, local(): lax.all_gather(attended, 'dp', axis=0, tiled=True)  7.11 us
    dot_general x1, matrix products, local(): jnp.dot(slices, joined, preferred_element_type=jnp.float32)  3.65 us
    convert_element_type x2, local copies, waits for them, and re-layouts, local(): projected = lax.all_to_all(episode_parts.astype(jnp.bfloat16), 'dp', spli...  3.5 us
  transfers between devices with their start and end apart: 1, of which 1 were waited for; matrix products, arithmetic and copies ran while one was open for 0% of the time, Pallas kernels for 0%

commit v1 on v0

--- a/solution.py
+++ b/solution.py
@@ -48,8 +48,11 @@
     stacked = jnp.transpose(query, (1, 0, 2)).reshape(num_heads * count, head_dim)
     rows_all = num_heads * count
     running_max = jnp.full((rows_all,), -1e30, jnp.float32)
-    key_piece = lax.all_gather(keys, "seq", axis=0, tiled=True)
-    value_piece = lax.all_gather(values, "seq", axis=0, tiled=True)
+    key_piece, value_piece = jnp.split(
+        lax.all_gather(jnp.concatenate([keys, values], axis=1), "seq", axis=0, tiled=True),
+        [keys.shape[1]],
+        axis=1,
+    )
     scores = lax.dot_general(
         stacked, key_piece, (((1,), (1,)), ((), ())), preferred_element_type=jnp.float32
     )

time: 117 us -> 112 us (0.957)
  blocking collectives: 65.8 us -> 24.1 us
  waiting for transfers between devices: 19.2 us -> 55.9 us
    all_gather x2 -> x0, blocking collectives: 41.7 us -> none  [the longest x1 22.9 us: local(): key_piece = lax.all_gather(keys, 'seq', axis=0, tiled=True)]
    all_gather x0 -> x1, waiting for transfers between devices: none -> 36.5 us  [local(): lax.all_gather(jnp.concatenate([keys, values], axis=1), 'seq', axis=0, ti...]
  transfers between devices with their start and end apart: 1 -> 2, of which waited for: 1 -> 2; matrix products, arithmetic and copies ran while one was open for 0% -> 1% of each run, Pallas kernels for 0% -> 0%
where the time goes in v1:
time: 112 us
  waiting for transfers between devices  55.9 us (50%)
  blocking collectives  24.1 us (22%)
  between operations  13.6 us (12%)
  local copies, waits for them, and re-layouts  7.77 us (7%)
  matrix products  6.15 us (5%)
  other arithmetic  4.17 us (4%)
    all_gather x1, waiting for transfers between devices, local(): lax.all_gather(jnp.concatenate([keys, values], axis=1), 'seq', axis=0, ti...  36.5 us
    reduce_scatter x1, waiting for transfers between devices, local(): lax.psum_scatter(jnp.dot(slices, joined, preferred_element_type=jnp.float...  19.4 us
    all_to_all x1, blocking collectives, local(): lax.all_to_all(normed, 'dp', split_axis=1, concat_axis=0, tiled=True)  9.24 us
    all_to_all x1, blocking collectives, local(): lax.all_to_all(episode_parts.astype(jnp.bfloat16), 'dp', split_axis=0, co...  7.85 us
    all_gather x1, blocking collectives, local(): lax.all_gather(attended, 'dp', axis=0, tiled=True)  6.99 us
    dot_general x1, matrix products, local(): jnp.dot(slices, joined, preferred_element_type=jnp.float32)  3.65 us
    convert_element_type x2, local copies, waits for them, and re-layouts, local(): projected = lax.all_to_all(episode_parts.astype(jnp.bfloat16), 'dp', spli...  2.69 us
  transfers between devices with their start and end apart: 2, of which 2 were waited for; matrix products, arithmetic and copies ran while one was open for 1% of the time, Pallas kernels for 0%

profile of v1, /device:TPU:0, one launch (start us, length us, event | category | flops | bytes accessed | tf_op | source)
XLA Modules:
  0.0 111.7 jit_solution(8430670939380911099)
XLA Ops:
  6.5 0.0 copy-start
  6.5 0.0 reduce-scatter.2.cloned.1.call-start
  6.5 1.3 %multiply_reduce_fusion = f32[64]{0:T(128)S(1)} fusion(bf16[1,64,2048]{2,1,0:T(8,128)(2,1)} %param.6), kind=kLoop, calls=%fused_computation.21 | loop fusion | flops 393152 | bytes 262400 | tf_op jit(solution)/shard_map/reduce_sum | solution.py:9
  7.8 1.5 %reshape.228 = f32[64,2,1024]{2,1,0:T(2,128)S(1)} reshape(bf16[1,64,2048]{2,1,0:T(8,128)(2,1)} %param.6) | data formatting | bytes 786432 | tf_op jit(solution)/shard_map/convert_element_type | solution.py:73
  9.3 0.7 mul.156
  10.0 0.3 multiply_convert_fusion
  10.4 9.2 %all_to_all.29 = bf16[64,2,1024]{2,0,1:T(8,128)(2,1)S(1)} all-to-all(bf16[64,2,1024]{2,0,1:T(8,128)(2,1)S(1)} %copy.15), channel_id=1, replica_groups=mesh['dp'=2,'seq'=16] {'dp'}, dimensions={1} | all-to-all | bytes 524288 | tf_op jit(solution)/shard_map/all_to_all | solution.py:32
  19.6 3.7 %fusion = f32[128,1792]{1,0:T(8,128)} fusion(bf16[128,1024]{1,0:T(8,128)(2,1)S(1)} %bitcast.26, bf16[1024,512]{1,0:T(8,128)(2,1)} %param.9, bf16[1024,1280]{1,0:T(8,128)(2,1)} %param.8), kind=kOutput, calls=%fused_computation | convolution fusion | flops 477102080 | bytes 4849664 | tf_op jit(solution)/shard_map/dot_general | solution.py:35
  23.3 0.0 reduce-scatter.2.cloned.1.call-update
  23.3 0.0 all-gather.2.cloned.1.call-start
  23.4 19.4 %reduce-scatter.2.cloned.1.call-done = f32[64,1792]{1,0:T(8,128)} async-done(((f32[128,1792]{1,0:T(8,128)}), f32[64,1792]{1,0:T(8,128)}) %reduce-scatter.2.cloned.1.call-update) | async-done | bytes 458768 | tf_op jit(solution)/shard_map/reduce_scatter | solution.py:34
  42.7 0.8 slice_bitcast_fusion
  43.6 0.2 fusion.20
  43.8 0.8 slice.49
  44.7 0.6 pad_maximum_fusion
  45.3 0.0 all-gather.2.cloned.1.call-update
  45.3 0.2 multiply_cosine_fusion.1
  45.5 1.0 slice.32
  46.5 0.1 reshape.226
  46.6 0.1 multiply_subtract_fusion
  46.7 0.1 fusion.14
  46.8 36.5 %all-gather.2.cloned.1.call-done = bf16[1024,512]{1,0:T(8,128)(2,1)} async-done(((bf16[64,512]{1,0:T(8,128)(2,1)}), bf16[1024,512]{1,0:T(8,128)(2,1)}) %all-gather.2.cloned.1.call-update) | async-done | bytes 1048592 | tf_op jit(solution)/shard_map/all_gather | solution.py:52
  83.3 0.0 copy-start.2
  83.3 1.6 %fusion.24 = (f32[320]{0:T(512)S(1)}, f32[320,1024]{1,0:T(8,128)S(1)}) fusion(bf16[320,256]{1,0:T(8,128)(2,1)S(1)} %bitcast.24, bf16[1024,512]{1,0:T(8,128)(2,1)} %all-gather.2.cloned.1.call-done), kind=kOutput, calls=%fused_computation.47 | convolution fusion | flops 168099520 | bytes 2000128 | tf_op jit(solution)/shard_map/dot_general | solution.py:56
  84.9 0.4 fusion.5
  85.3 0.0 copy-done.2
  85.3 0.4 fusion.4
  85.7 7.0 %all_gather.7 = bf16[128,1280]{1,0:T(8,128)(2,1)S(1)} all-gather(bf16[64,1280]{1,0:T(8,128)(2,1)S(1)} %bitcast.25), channel_id=1, replica_groups=mesh['dp'=2,'seq'=16] {'dp'}, dimensions={0}, use_global_device_ids=true | all-gather | bytes 491520 | tf_op jit(solution)/shard_map/all_gather | solution.py:66
  92.7 0.0 copy-done
  92.7 0.5 convolution_convert_fusion
  93.2 0.0 copy-start.1
  93.2 0.0 copy-start.3
  93.2 7.8 %all_to_all.30 = bf16[2,64,1024]{2,1,0:T(8,128)(2,1)S(1)} all-to-all(bf16[2,64,1024]{2,1,0:T(8,128)(2,1)S(1)} %bitcast.23), channel_id=1, replica_groups=mesh['dp'=2,'seq'=16] {'dp'}, dimensions={0} | all-to-all | bytes 524288 | tf_op jit(solution)/shard_map/all_to_all | solution.py:70
  101.1 0.2 fusion.9
  101.3 1.2 %copy.18 = f32[64,2,1024]{2,1,0:T(2,128)} copy(f32[64,2,1024]{2,0,1:T(8,128)S(1)} %convert_bitcast_fusion) | data formatting | bytes 1048576 | tf_op jit(solution)/shard_map/convert_element_type | solution.py:72
  102.5 1.5 %reshape.229 = f32[1,64,2048]{2,1,0:T(8,128)S(1)} reshape(f32[64,2,1024]{2,1,0:T(2,128)} %copy.18) | data formatting | bytes 1048576 | tf_op jit(solution)/shard_map/convert_element_type | solution.py:72
  104.0 0.0 copy-done.1
  104.0 0.0 copy-done.3
  104.0 0.9 add_convert_fusion
  (10 shorter events, 0.2 us)
Async XLA Ops:
  6.5 86.2 %copy-start = (bf16[1280,1024]{1,0:T(8,128)(2,1)S(1)}, bf16[1280,1024]{1,0:T(8,128)(2,1)}, u32[]{:S(2)}) copy-start(bf16[1280,1024]{1,0:T(8,128)(2,1)} %param.10) | copy-start | bytes 7864324
  6.5 36.2 %reduce-scatter.2.cloned.1.call-start = ((), (), s32[]{:S(2)}) async-start(), calls=%async_computation.3 | async-start | bytes 1376256 | tf_op jit(solution)/shard_map/reduce_scatter | solution.py:34
  23.3 60.0 %all-gather.2.cloned.1.call-start = ((), (), s32[]{:S(2)}) async-start(), calls=%async_computation.4 | async-start | bytes 1114112 | tf_op jit(solution)/shard_map/all_gather | solution.py:52
  83.3 2.0 %copy-start.2 = (bf16[1024,512]{1,0:T(8,128)(2,1)S(1)}, bf16[1024,512]{1,0:T(8,128)(2,1)}, u32[]{:S(2)}) copy-start(bf16[1024,512]{1,0:T(8,128)(2,1)} %all-gather.2.cloned.1.call-done) | copy-start | bytes 3145732
  93.2 10.8 %copy-start.1 = (bf16[1,64,2048]{2,1,0:T(8,128)(2,1)S(1)}, bf16[1,64,2048]{2,1,0:T(8,128)(2,1)}, u32[]{:S(2)}) copy-start(bf16[1,64,2048]{2,1,0:T(8,128)(2,1)} %param.6) | copy-start | bytes 786436
  93.2 10.8 %copy-start.3 = (f32[2048]{0:T(1024)S(1)}, f32[2048]{0:T(1024)}, u32[]{:S(2)}) copy-start(f32[2048]{0:T(1024)} %param.11) | copy-start | bytes 24580
Sparse Core Ops, SparseCore 0:
  23.4 19.2 reduce-scatter.1
  45.4 37.8 all-gather.1
